TPU v7x, 512 devices: a whole 4x4x16 slice. The times are simulated.
512 devices in a mesh: obs: 16 (over z_hi, y, core), flux: 32 (over z_lo, x).
Axes of the slice: x: 4, y: 4, z: 16 (z_hi: 2, z_lo: 8; z = z_hi * 8 + z_lo), core: 2. Of those that a mesh axis runs over, the one named last changes fastest.
Arguments:
- jacobian: bfloat16 [2048, 32768], P('obs', 'flux'), may hold values from -0.03125 to 0.03125
- probes: bfloat16 [2, 32768, 128], P(None, 'flux'), may hold values from -6 to 6
- prior_std: float32 [32768], P('flux'), may hold values from 0.5 to 2
- obs_weight: float32 [2048], P('obs'), may hold values from 0.25 to 4
Outputs:
- sketch: float32 [32768, 256], P(('flux', 'obs'))
- basis_out: float32 [32768, 256], P(('flux', 'obs'))
All inputs are finite; a program needn't handle non-finite values.
Results may differ from a plain program's by a relative error of at most 0.005.
Values may be sent and summed in bfloat16 or wider, within the bound.
No kernel may reach another device: no remote copies, remote signals or barrier semaphores. Data moves between devices by JAX's collectives and lax.ppermute only.
A program may use at most 64 MiB of HBM per device.

v0:
```python
import functools
import math

import jax
import jax.numpy as jnp
from jax import lax
from jax.experimental import pallas as pl
from jax.experimental.pallas import tpu as pltpu
from jax.sharding import Mesh, PartitionSpec as P

OBS_AXES = ("zh", "y", "c")
FLUX_AXES = ("zl", "x")
NEAR_OBS = ("y", "c")
PLANE = ("y", "c", "x")
LINE = ("zh", "zl")
HALF = 128
STEP = 8
VMEM_LIMIT = 16 * 2**20
HIGHEST = lax.Precision.HIGHEST


def pick(values, index):
    return jnp.take_along_axis(values, index, axis=1, mode="promise_in_bounds")


def eliminate(diag, side, inverse, lanes, near):
    sub = lax.broadcasted_iota(jnp.int32, (STEP, HALF), 0)
    blocks = HALF // STEP
    columns = [pick(diag[:STEP, :], jnp.full((STEP, HALF), k, jnp.int32)) for k in range(STEP)]
    for t in range(blocks):
        top, low = t * STEP, (t + 1) * STEP
        base = t % 2 * STEP * STEP
        for k in range(STEP):
            lanes[base + k * STEP : base + (k + 1) * STEP, :] = columns[k]
        entry = {}
        for k in range(STEP):
            for j in range(k, STEP):
                entry[j, k] = lanes[pl.ds(base + k * STEP + j, STEP, stride=0), :]
        rows = [[ref[pl.ds(top + k, STEP, stride=0), :] for ref in (diag, side, inverse)] for k in range(STEP)]
        last = t + 1 == blocks
        if not last:
            below = diag[low : low + STEP, :]
            columns = [pick(below, jnp.full((STEP, HALF), low + k, jnp.int32)) for k in range(STEP)]
        for k in range(STEP):
            scale = lax.rsqrt(entry[k, k])
            rows[k] = [row * scale for row in rows[k]]
            mult = {j: entry[j, k] * scale for j in range(k + 1, STEP)}
            for j in range(k + 1, STEP):
                for i in range(j, STEP):
                    entry[i, j] = entry[i, j] - mult[i] * mult[j]
                rows[j] = [row - mult[j] * pivot for row, pivot in zip(rows[j], rows[k])]
            for ref, row in zip((side, inverse), rows[k][1:]):
                ref[top + k : top + k + 1, :] = row[:1, :]
            if not last:
                mult = pick(rows[k][0], sub + low)
                spot = base + k * STEP
                near[spot : spot + STEP, :] = mult
                columns = [
                    column - mult * near[pl.ds(spot + j, STEP, stride=0), :]
                    for j, column in enumerate(columns)
                ]
        for block in range(t + 1, blocks):
            low = block * STEP
            index = sub + low
            work = [ref[low : low + STEP, :] for ref in (diag, side, inverse)]
            for k in range(STEP):
                if block == t + 1:
                    mult = near[base + k * STEP : base + (k + 1) * STEP, :]
                else:
                    mult = pick(rows[k][0], index)
                work = [row - mult * pivot for row, pivot in zip(work, rows[k])]
            for ref, row in zip((diag, side, inverse), work):
                ref[low : low + STEP, :] = row


def identity():
    shape = (HALF, HALF)
    return (lax.broadcasted_iota(jnp.int32, shape, 0) == lax.broadcasted_iota(jnp.int32, shape, 1)).astype(jnp.float32)


def dot(a, b, dims):
    return lax.dot_general(a, b, (dims, ((), ())), precision=HIGHEST, preferred_element_type=jnp.float32)


def basis_kernel(root, gram, sketch, out, diag, side, low, mixed, high, lanes, near):
    diag[...] = gram[:HALF, :HALF]
    side[...] = gram[:HALF, HALF:]
    low[...] = identity()
    eliminate(diag, side, low, lanes, near)
    upper = side[...]
    diag[...] = gram[HALF:, HALF:] - dot(upper, upper, ((0,), (0,)))
    mixed[...] = -dot(upper, low[...], ((0,), (0,)))
    high[...] = identity()
    eliminate(diag, mixed, high, lanes, near)
    first, second = sketch[:, :HALF], sketch[:, HALF:]
    out[:, :HALF] = root * dot(first, low[...], ((1,), (1,)))
    out[:, HALF:] = root * (dot(first, mixed[...], ((1,), (1,))) + dot(second, high[...], ((1,), (1,))))


def basis(gram, sketch, root):
    square = pltpu.VMEM((HALF, HALF), jnp.float32)
    vmem = pl.BlockSpec(memory_space=pltpu.VMEM)
    return pl.pallas_call(
        functools.partial(basis_kernel, root),
        out_shape=jax.ShapeDtypeStruct(sketch.shape, jnp.float32),
        in_specs=[vmem, vmem],
        out_specs=vmem,
        scratch_shapes=[square, square, square, square, square, *[pltpu.VMEM((2 * STEP * STEP, HALF), jnp.float32)] * 2],
        compiler_params=pltpu.CompilerParams(vmem_limit_bytes=VMEM_LIMIT),
        name="cholesky_basis",
    )(gram, sketch)


def forward_kernel(jacobian, probes, spread, out, stacked):
    sub = lax.broadcasted_iota(jnp.int32, (STEP, HALF), 0)
    blocks, flux_local, _ = probes.shape
    pair = 2 * STEP
    for low in range(0, flux_local, pair):
        row = spread[pl.ds(low // HALF, STEP, stride=0), :]
        factor = jnp.concatenate([pick(row, sub + (low + half) % HALF) for half in (0, STEP)], axis=0)
        for b in range(blocks):
            scaled = probes[b, low : low + pair, :].astype(jnp.float32) * factor
            stacked[low : low + pair, b * HALF : (b + 1) * HALF] = scaled.astype(jnp.bfloat16)
    total = jnp.dot(jacobian[...], stacked[...], preferred_element_type=jnp.float32)
    for k in range(out.shape[0]):
        r, c = k // blocks * STEP, k % blocks * HALF
        out[k] = total[r : r + STEP, c : c + HALF]


def forward_tiles(jacobian, probes, prior_std):
    rows, flux_local = jacobian.shape
    columns = probes.shape[0] * probes.shape[2]
    vmem = pl.BlockSpec(memory_space=pltpu.VMEM)
    return pl.pallas_call(
        forward_kernel,
        out_shape=jax.ShapeDtypeStruct((rows * columns // (STEP * HALF), STEP, HALF), jnp.float32),
        in_specs=[vmem, vmem, vmem],
        out_specs=vmem,
        scratch_shapes=[pltpu.VMEM((flux_local, columns), jnp.bfloat16)],
        name="forward_tiles",
    )(jacobian, probes, prior_std.reshape(flux_local // HALF, HALF))


def scatter_sum(parts, axes):
    moved = lax.all_to_all(parts, axes, 0, 0, tiled=True)
    return jnp.sum(moved.astype(jnp.float32), axis=0)


def gather(piece, axes):
    count = lax.axis_size(axes)
    return lax.all_to_all(
        jnp.broadcast_to(piece[None], (count, *piece.shape)), axes, 0, 0, tiled=True
    )


def from_tiles(tiles, rows, cols):
    return tiles.reshape(rows // 8, cols // 128, 8, 128).transpose(0, 2, 1, 3).reshape(rows, cols)


def pull(jacobian, weighted):
    return lax.dot_general(
        jacobian, weighted, (((0,), (0,)), ((), ())), preferred_element_type=jnp.float32
    )


def body(jacobian, probes, prior_std, obs_weight):
    flux_local = probes.shape[1]
    obs_local = jacobian.shape[0]
    columns = probes.shape[0] * probes.shape[2]
    half, far = flux_local // 2, lax.axis_index("zh").astype(jnp.uint32)
    rows = (far * obs_local, (1 - far) * obs_local, far * half)
    portion = flux_local // lax.axis_size(OBS_AXES)
    local_std = lax.dynamic_slice_in_dim(prior_std, lax.axis_index(OBS_AXES) * portion, portion)
    row = lax.axis_index(FLUX_AXES) // (columns // 128) * 8
    weight = lax.dynamic_slice_in_dim(obs_weight, row, 8)
    sent = lax.dynamic_slice_in_dim(jacobian, (1 - far) * half, half, 1)
    far_part = lax.ppermute(sent, "zh", ((0, 1), (1, 0)))
    tiles = forward_tiles(jacobian, probes, prior_std)
    moved = lax.all_to_all(tiles, FLUX_AXES, 0, 0, tiled=True)
    tile = jnp.sum(moved, axis=0)
    tile, weight, local_std, rows = lax.optimization_barrier((tile, weight, local_std, rows))
    near_part = lax.dynamic_slice_in_dim(jacobian, rows[2], half, 1)
    weighted = gather((tile * weight[:, None]).astype(jnp.bfloat16), ("zh",) + FLUX_AXES)
    weighted = from_tiles(weighted, 2 * obs_local, columns)
    adjoint = pull(near_part, lax.dynamic_slice_in_dim(weighted, rows[0], obs_local))
    adjoint += pull(far_part, lax.dynamic_slice_in_dim(weighted, rows[1], obs_local))
    adjoint = scatter_sum(adjoint.astype(jnp.bfloat16).reshape(-1, portion, columns), NEAR_OBS)
    sketch = adjoint * local_std[:, None]
    gram = jnp.dot(
        sketch.T, sketch, precision=lax.Precision.HIGHEST, preferred_element_type=jnp.float32
    )
    slab = scatter_sum(gram.astype(jnp.bfloat16).reshape(lax.axis_size(PLANE), -1, columns), PLANE)
    slab = lax.optimization_barrier(slab).astype(jnp.bfloat16)
    slab = jnp.sum(gather(slab, LINE).astype(jnp.float32), axis=0)
    gram = gather(slab, PLANE).reshape(columns, columns)
    scale_root = math.sqrt(flux_local * lax.axis_size(FLUX_AXES))
    return (sketch, basis(gram, sketch, scale_root))


def solution(mesh):
    split = Mesh(mesh.devices.reshape(2, 4, 2, 8, 4), ("zh", "y", "c", "zl", "x"))
    in_specs = (P(OBS_AXES, FLUX_AXES), P(None, FLUX_AXES, None), P(FLUX_AXES), P(OBS_AXES))
    out_specs = (P(FLUX_AXES + OBS_AXES, None), P(FLUX_AXES + OBS_AXES, None))

    return jax.shard_map(body, mesh=split, in_specs=in_specs, out_specs=out_specs, check_vma=False)
```

profile of v0, /device:TPU:1, one launch (start us, length us, event | category | flops | bytes accessed | tf_op | source)
XLA Modules:
  0.0 134.6 jit_solution(1372798112056242306)
XLA Ops:
  0.6 2.4 %forward_tiles.1 = f32[32,8,128]{2,1,0:T(8,128)} custom-call(bf16[128,1024]{1,0:T(8,128)(2,1)} %jacobian.1, bf16[2,1024,128]{2,1,0:T(8,128)(2,1)} %probes.1, f32[8,128]{1,0:T(8,128)} %bitcast.17), custom_call_target="tpu_custom_call" | custom-call | tf_op jit(solution)/shard_map/forward_tiles/pallas_call | solution.py:134
  3.0 15.9 %all-to-all-start = ((f32[32,8,128]{2,1,0:T(8,128)}), f32[32,8,128]{2,1,0:T(8,128)S(1)}, u32[]{:S(2)}, u32[]{:S(2)}) async-start(f32[32,8,128]{2,1,0:T(8,128)} %forward_tiles.1), calls=%async_computation | async-start | bytes 262144 | tf_op jit(solution)/shard_map/all_to_all | solution.py:179
  19.0 0.8 dynamic_slice.19
  19.7 0.0 copy-start.2
  19.7 0.7 copy-done.2
  20.4 0.1 dynamic_slice.18
  20.4 0.0 copy-start.1
  20.5 10.6 %all-to-all-done = f32[32,8,128]{2,1,0:T(8,128)S(1)} async-done(((f32[32,8,128]{2,1,0:T(8,128)}), f32[32,8,128]{2,1,0:T(8,128)S(1)}, u32[]{:S(2)}, u32[]{:S(2)}) %all-to-all-start) | async-done | bytes 131104 | tf_op jit(solution)/shard_map/all_to_all | solution.py:179
  31.1 0.1 multiply_convert_fusion
  31.2 0.7 broadcast_in_dim.6
  31.8 9.4 %all-to-all-start.1 = ((bf16[64,8,128]{2,1,0:T(8,128)(2,1)}), bf16[64,8,128]{2,1,0:T(8,128)(2,1)S(1)}, u32[]{:S(2)}, u32[]{:S(2)}) async-start(bf16[64,8,128]{2,1,0:T(8,128)(2,1)} %broadcast_in_dim.6), calls=%async_computation.1 | async-start | bytes 262144 | tf_op jit(solution)/shard_map/all_to_all | solution.py:151
  41.3 0.0 copy-done.1
  41.3 11.7 %collective-permute-start = (bf16[128,512]{1,0:T(8,128)(2,1)S(1)}, bf16[128,512]{1,0:T(8,128)(2,1)S(1)}, u32[]{:S(2)}, u32[]{:S(2)}) collective-permute-start(bf16[128,512]{1,0:T(8,128)(2,1)S(1)} %constant_dynamic-slice_fusion), channel_id=1, source_target_pairs={{0,256},{256,0},{1,257},{257,1},{2,258},{258,2},{3,259},{259,3},{4... | collective-permute-start | bytes 393224 | tf_op jit(solution)/shard_map/ppermute | solution.py:177
  53.0 3.2 %all-to-all-done.1 = bf16[64,8,128]{2,1,0:T(8,128)(2,1)S(1)} async-done(((bf16[64,8,128]{2,1,0:T(8,128)(2,1)}), bf16[64,8,128]{2,1,0:T(8,128)(2,1)S(1)}, u32[]{:S(2)}, u32[]{:S(2)}) %all-to-all-start.1) | async-done | bytes 131104 | tf_op jit(solution)/shard_map/all_to_all | solution.py:151
  56.3 0.3 fusion.2
  56.6 10.0 %collective-permute-done = bf16[128,512]{1,0:T(8,128)(2,1)S(1)} collective-permute-done((bf16[128,512]{1,0:T(8,128)(2,1)S(1)}, bf16[128,512]{1,0:T(8,128)(2,1)S(1)}, u32[]{:S(2)}, u32[]{:S(2)}) %collective-permute-start) | collective-permute-done | bytes 131104 | tf_op jit(solution)/shard_map/ppermute | solution.py:177
  66.6 0.2 fusion
  66.9 12.6 %all_to_all.30 = bf16[8,64,256]{2,1,0:T(8,128)(2,1)S(1)} all-to-all(bf16[8,64,256]{2,1,0:T(8,128)(2,1)S(1)} %bitcast.14), channel_id=1, replica_groups=mesh['zh'=2,'y'=4,'c'=2,'zl'=8,'x'=4] {'y','c'}, dimensions={0} | all-to-all | bytes 524288 | tf_op jit(solution)/shard_map/all_to_all | solution.py:145
  79.5 0.1 broadcast_multiply_fusion.sketch
  79.6 0.0 copy-start
  79.6 0.4 fusion.1
  80.0 13.3 %all_to_all.31 = bf16[32,8,256]{2,1,0:T(8,128)(2,1)S(1)} all-to-all(bf16[32,8,256]{2,1,0:T(8,128)(2,1)S(1)} %fusion.1), channel_id=1, replica_groups=mesh['zh'=2,'y'=4,'c'=2,'zl'=8,'x'=4] {'y','c','x'}, dimensions={0} | all-to-all | bytes 262144 | tf_op jit(solution)/shard_map/all_to_all | solution.py:145
  93.4 19.7 %all_to_all.32 = bf16[16,8,256]{2,1,0:T(8,128)(2,1)S(1)} all-to-all(bf16[16,8,256]{2,1,0:T(8,128)(2,1)S(1)} %broadcast_in_dim.7), channel_id=1, replica_groups=mesh['zh'=2,'y'=4,'c'=2,'zl'=8,'x'=4] {'zh','zl'}, dimensions={0} | all-to-all | bytes 131072 | tf_op jit(solution)/shard_map/all_to_all | solution.py:151
  113.1 14.2 %all_to_all.33 = f32[32,8,256]{2,1,0:T(8,128)S(1)} all-to-all(f32[32,8,256]{2,1,0:T(8,128)S(1)} %broadcast_in_dim.8), channel_id=1, replica_groups=mesh['zh'=2,'y'=4,'c'=2,'zl'=8,'x'=4] {'y','c','x'}, dimensions={0} | all-to-all | bytes 524288 | tf_op jit(solution)/shard_map/all_to_all | solution.py:151
  127.4 0.0 copy-done
  127.4 7.2 %cholesky_basis.1 = f32[64,256]{1,0:T(8,128)} custom-call(f32[256,256]{1,0:T(8,128)S(1)} %bitcast.13, f32[64,256]{1,0:T(8,128)S(1)} %broadcast_multiply_fusion.sketch), custom_call_target="tpu_custom_call" | custom-call | tf_op jit(solution)/shard_map/cholesky_basis/pallas_call | solution.py:103
  (7 shorter events, 0.2 us)
Async XLA Ops:
  3.0 28.0 %all-to-all-start = ((f32[32,8,128]{2,1,0:T(8,128)}), f32[32,8,128]{2,1,0:T(8,128)S(1)}, u32[]{:S(2)}, u32[]{:S(2)}) async-start(f32[32,8,128]{2,1,0:T(8,128)} %forward_tiles.1), calls=%async_computation | async-start | bytes 262144 | tf_op jit(solution)/shard_map/all_to_all | solution.py:179
  19.7 0.7 copy-start.2
  20.4 20.8 %copy-start.1 = (bf16[128,1024]{1,0:T(8,128)(2,1)S(1)}, bf16[128,1024]{1,0:T(8,128)(2,1)}, u32[]{:S(2)}) copy-start(bf16[128,1024]{1,0:T(8,128)(2,1)} %jacobian.1) | copy-start | bytes 786436
  31.8 24.4 %all-to-all-start.1 = ((bf16[64,8,128]{2,1,0:T(8,128)(2,1)}), bf16[64,8,128]{2,1,0:T(8,128)(2,1)S(1)}, u32[]{:S(2)}, u32[]{:S(2)}) async-start(bf16[64,8,128]{2,1,0:T(8,128)(2,1)} %broadcast_in_dim.6), calls=%async_computation.1 | async-start | bytes 262144 | tf_op jit(solution)/shard_map/all_to_all | solution.py:151
  41.3 25.3 %collective-permute-start = (bf16[128,512]{1,0:T(8,128)(2,1)S(1)}, bf16[128,512]{1,0:T(8,128)(2,1)S(1)}, u32[]{:S(2)}, u32[]{:S(2)}) collective-permute-start(bf16[128,512]{1,0:T(8,128)(2,1)S(1)} %constant_dynamic-slice_fusion), channel_id=1, source_target_pairs={{0,256},{256,0},{1,257},{257,1},{2,258},{258,2},{3,259},{259,3},{4... | collective-permute-start | bytes 393224 | tf_op jit(solution)/shard_map/ppermute | solution.py:177
  79.6 47.7 %copy-start = (f32[64,256]{1,0:T(8,128)}, f32[64,256]{1,0:T(8,128)S(1)}, u32[]{:S(2)}) copy-start(f32[64,256]{1,0:T(8,128)S(1)} %broadcast_multiply_fusion.sketch) | copy-start | bytes 196612
where the time goes:
time: 135 us
  blocking collectives  59.8 us (44%)
  starting transfers between devices  37.1 us (27%)
  waiting for transfers between devices  23.9 us (18%)
  Pallas kernels  9.62 us (7%)
  local copies, waits for them, and re-layouts  2.2 us (2%)
    all_to_all x2, blocking collectives, gather(): lax.all_to_all(jnp.broadcast_to(piece[None], (count, *piece.shape)), axes...  33.9 us
    all_to_all x2, blocking collectives, scatter_sum(): moved = lax.all_to_all(parts, axes, 0, 0, tiled=True)  25.9 us
    all_to_all x1, starting transfers between devices, body(): moved = lax.all_to_all(tiles, FLUX_AXES, 0, 0, tiled=True)  15.9 us
    ppermute x1, starting transfers between devices, body(): far_part = lax.ppermute(sent, 'zh', ((0, 1), (1, 0)))  11.7 us
    all_to_all x1, waiting for transfers between devices, body(): moved = lax.all_to_all(tiles, FLUX_AXES, 0, 0, tiled=True)  10.6 us
    ppermute x1, waiting for transfers between devices, body(): far_part = lax.ppermute(sent, 'zh', ((0, 1), (1, 0)))  10 us
    all_to_all x1, starting transfers between devices, gather(): lax.all_to_all(jnp.broadcast_to(piece[None], (count, *piece.shape)), axes...  9.43 us
    pallas_call x1, Pallas kernels, basis(): pl.pallas_call(functools.partial(basis_kernel, root), out_shape=jax.Shape...  7.24 us
  transfers between devices with their start and end apart: 3, of which 3 were waited for; matrix products, arithmetic and copies ran while one was open for 1% of the time, Pallas kernels for 0%

commit v1 on v0

--- a/solution.py
+++ b/solution.py
@@ -15,6 +15,7 @@
 LINE = ("zh", "zl")
 HALF = 128
 STEP = 8
+CHUNKS = 4
 VMEM_LIMIT = 16 * 2**20
 HIGHEST = lax.Precision.HIGHEST
 
@@ -23,7 +24,7 @@
     return jnp.take_along_axis(values, index, axis=1, mode="promise_in_bounds")
 
 
-def eliminate(diag, side, inverse, lanes, near):
+def eliminate(diag, inverse, lanes, near):
     sub = lax.broadcasted_iota(jnp.int32, (STEP, HALF), 0)
     blocks = HALF // STEP
     columns = [pick(diag[:STEP, :], jnp.full((STEP, HALF), k, jnp.int32)) for k in range(STEP)]
@@ -36,7 +37,7 @@
         for k in range(STEP):
             for j in range(k, STEP):
                 entry[j, k] = lanes[pl.ds(base + k * STEP + j, STEP, stride=0), :]
-        rows = [[ref[pl.ds(top + k, STEP, stride=0), :] for ref in (diag, side, inverse)] for k in range(STEP)]
+        rows = [[ref[pl.ds(top + k, STEP, stride=0), :] for ref in (diag, inverse)] for k in range(STEP)]
         last = t + 1 == blocks
         if not last:
             below = diag[low : low + STEP, :]
@@ -49,7 +50,7 @@
                 for i in range(j, STEP):
                     entry[i, j] = entry[i, j] - mult[i] * mult[j]
                 rows[j] = [row - mult[j] * pivot for row, pivot in zip(rows[j], rows[k])]
-            for ref, row in zip((side, inverse), rows[k][1:]):
+            for ref, row in zip((inverse,), rows[k][1:]):
                 ref[top + k : top + k + 1, :] = row[:1, :]
             if not last:
                 mult = pick(rows[k][0], sub + low)
@@ -62,14 +63,14 @@
         for block in range(t + 1, blocks):
             low = block * STEP
             index = sub + low
-            work = [ref[low : low + STEP, :] for ref in (diag, side, inverse)]
+            work = [ref[low : low + STEP, :] for ref in (diag, inverse)]
             for k in range(STEP):
                 if block == t + 1:
                     mult = near[base + k * STEP : base + (k + 1) * STEP, :]
                 else:
                     mult = pick(rows[k][0], index)
                 work = [row - mult * pivot for row, pivot in zip(work, rows[k])]
-            for ref, row in zip((diag, side, inverse), work):
+            for ref, row in zip((diag, inverse), work):
                 ref[low : low + STEP, :] = row
 
 
@@ -82,19 +83,19 @@
     return lax.dot_general(a, b, (dims, ((), ())), precision=HIGHEST, preferred_element_type=jnp.float32)
 
 
-def basis_kernel(root, gram, sketch, out, diag, side, low, mixed, high, lanes, near):
+def basis_kernel(root, gram, sketch, out, diag, low, high, lanes, near):
     diag[...] = gram[:HALF, :HALF]
-    side[...] = gram[:HALF, HALF:]
     low[...] = identity()
-    eliminate(diag, side, low, lanes, near)
-    upper = side[...]
+    eliminate(diag, low, lanes, near)
+    upper = dot(low[...], gram[:HALF, HALF:], ((1,), (0,)))
     diag[...] = gram[HALF:, HALF:] - dot(upper, upper, ((0,), (0,)))
-    mixed[...] = -dot(upper, low[...], ((0,), (0,)))
     high[...] = identity()
-    eliminate(diag, mixed, high, lanes, near)
+    eliminate(diag, high, lanes, near)
     first, second = sketch[:, :HALF], sketch[:, HALF:]
-    out[:, :HALF] = root * dot(first, low[...], ((1,), (1,)))
-    out[:, HALF:] = root * (dot(first, mixed[...], ((1,), (1,))) + dot(second, high[...], ((1,), (1,))))
+    left = dot(first, low[...], ((1,), (1,)))
+    out[:, :HALF] = root * left
+    rest = second - dot(left, upper, ((1,), (0,)))
+    out[:, HALF:] = root * dot(rest, high[...], ((1,), (1,)))
 
 
 def basis(gram, sketch, root):
@@ -105,40 +106,69 @@
         out_shape=jax.ShapeDtypeStruct(sketch.shape, jnp.float32),
         in_specs=[vmem, vmem],
         out_specs=vmem,
-        scratch_shapes=[square, square, square, square, square, *[pltpu.VMEM((2 * STEP * STEP, HALF), jnp.float32)] * 2],
+        scratch_shapes=[square, square, square, *[pltpu.VMEM((2 * STEP * STEP, HALF), jnp.float32)] * 2],
         compiler_params=pltpu.CompilerParams(vmem_limit_bytes=VMEM_LIMIT),
         name="cholesky_basis",
     )(gram, sketch)
 
 
-def forward_kernel(jacobian, probes, spread, out, stacked):
+def forward_kernel(
+    far_jacobian, far_probes, far_spread, far_weight, far_out, jacobian, probes, spread, weight, stacked, out, sems
+):
     sub = lax.broadcasted_iota(jnp.int32, (STEP, HALF), 0)
     blocks, flux_local, _ = probes.shape
-    pair = 2 * STEP
+    pair, chunk = 2 * STEP, flux_local // CHUNKS
+    copies = [pltpu.make_async_copy(far_spread, spread, sems.at[CHUNKS])]
+    for c in range(CHUNKS):
+        part = (slice(None), pl.ds(c * chunk, chunk), slice(None))
+        copies.append(pltpu.make_async_copy(far_probes.at[part], probes.at[part], sems.at[c]))
+    copies.append(pltpu.make_async_copy(far_weight, weight, sems.at[CHUNKS + 2]))
+    copies.append(pltpu.make_async_copy(far_jacobian, jacobian, sems.at[CHUNKS + 1]))
+    for copy in copies:
+        copy.start()
+    copies[0].wait()
     for low in range(0, flux_local, pair):
+        if low % chunk == 0:
+            copies[1 + low // chunk].wait()
         row = spread[pl.ds(low // HALF, STEP, stride=0), :]
         factor = jnp.concatenate([pick(row, sub + (low + half) % HALF) for half in (0, STEP)], axis=0)
         for b in range(blocks):
             scaled = probes[b, low : low + pair, :].astype(jnp.float32) * factor
             stacked[low : low + pair, b * HALF : (b + 1) * HALF] = scaled.astype(jnp.bfloat16)
+    copies[-2].wait()
+    row = weight[pl.ds(0, STEP, stride=0), :]
+    copies[-1].wait()
     total = jnp.dot(jacobian[...], stacked[...], preferred_element_type=jnp.float32)
     for k in range(out.shape[0]):
         r, c = k // blocks * STEP, k % blocks * HALF
-        out[k] = total[r : r + STEP, c : c + HALF]
-
-
-def forward_tiles(jacobian, probes, prior_std):
+        out[k] = total[r : r + STEP, c : c + HALF] * pick(row, sub + r)
+    result = pltpu.make_async_copy(out, far_out, sems.at[CHUNKS])
+    result.start()
+    result.wait()
+
+
+def forward_tiles(jacobian, probes, prior_std, obs_weight):
     rows, flux_local = jacobian.shape
     columns = probes.shape[0] * probes.shape[2]
-    vmem = pl.BlockSpec(memory_space=pltpu.VMEM)
+    spread = prior_std.reshape(flux_local // HALF, HALF)
+    hbm = pl.BlockSpec(memory_space=pltpu.MemorySpace.HBM)
+    shape = (rows * columns // (STEP * HALF), STEP, HALF)
     return pl.pallas_call(
         forward_kernel,
-        out_shape=jax.ShapeDtypeStruct((rows * columns // (STEP * HALF), STEP, HALF), jnp.float32),
-        in_specs=[vmem, vmem, vmem],
-        out_specs=vmem,
-        scratch_shapes=[pltpu.VMEM((flux_local, columns), jnp.bfloat16)],
+        out_shape=jax.ShapeDtypeStruct(shape, jnp.float32),
+        in_specs=[hbm] * 4,
+        out_specs=hbm,
+        scratch_shapes=[
+            pltpu.VMEM(jacobian.shape, jacobian.dtype),
+            pltpu.VMEM(probes.shape, probes.dtype),
+            pltpu.VMEM(spread.shape, spread.dtype),
+            pltpu.VMEM((1, rows), jnp.float32),
+            pltpu.VMEM((flux_local, columns), jnp.bfloat16),
+            pltpu.VMEM(shape, jnp.float32),
+            pltpu.SemaphoreType.DMA((CHUNKS + 3,)),
+        ],
         name="forward_tiles",
-    )(jacobian, probes, prior_std.reshape(flux_local // HALF, HALF))
+    )(jacobian, probes, spread, obs_weight.reshape(1, rows))
 
 
 def scatter_sum(parts, axes):
@@ -171,16 +201,14 @@
     rows = (far * obs_local, (1 - far) * obs_local, far * half)
     portion = flux_local // lax.axis_size(OBS_AXES)
     local_std = lax.dynamic_slice_in_dim(prior_std, lax.axis_index(OBS_AXES) * portion, portion)
-    row = lax.axis_index(FLUX_AXES) // (columns // 128) * 8
-    weight = lax.dynamic_slice_in_dim(obs_weight, row, 8)
     sent = lax.dynamic_slice_in_dim(jacobian, (1 - far) * half, half, 1)
     far_part = lax.ppermute(sent, "zh", ((0, 1), (1, 0)))
-    tiles = forward_tiles(jacobian, probes, prior_std)
+    tiles = forward_tiles(jacobian, probes, prior_std, obs_weight)
     moved = lax.all_to_all(tiles, FLUX_AXES, 0, 0, tiled=True)
     tile = jnp.sum(moved, axis=0)
-    tile, weight, local_std, rows = lax.optimization_barrier((tile, weight, local_std, rows))
+    tile, local_std, rows = lax.optimization_barrier((tile, local_std, rows))
     near_part = lax.dynamic_slice_in_dim(jacobian, rows[2], half, 1)
-    weighted = gather((tile * weight[:, None]).astype(jnp.bfloat16), ("zh",) + FLUX_AXES)
+    weighted = gather(tile.astype(jnp.bfloat16), ("zh",) + FLUX_AXES)
     weighted = from_tiles(weighted, 2 * obs_local, columns)
     adjoint = pull(near_part, lax.dynamic_slice_in_dim(weighted, rows[0], obs_local))
     adjoint += pull(far_part, lax.dynamic_slice_in_dim(weighted, rows[1], obs_local))

time: 135 us -> 135 us (level)
  no operation moved by 1% of the time
where the time goes in v1:
time: 135 us; the launch traced here: 134 us
  blocking collectives  59.8 us (44%)
  starting transfers between devices  37.1 us (27%)
  waiting for transfers between devices  24.6 us (18%)
  Pallas kernels  9.54 us (7%)
  local copies, waits for them, and re-layouts  1.47 us (1%)
    all_to_all x2, blocking collectives, gather(): lax.all_to_all(jnp.broadcast_to(piece[None], (count, *piece.shape)), axes...  33.9 us
    all_to_all x2, blocking collectives, scatter_sum(): moved = lax.all_to_all(parts, axes, 0, 0, tiled=True)  25.9 us
    all_to_all x1, starting transfers between devices, body(): moved = lax.all_to_all(tiles, FLUX_AXES, 0, 0, tiled=True)  15.9 us
    ppermute x1, starting transfers between devices, body(): far_part = lax.ppermute(sent, 'zh', ((0, 1), (1, 0)))  11.7 us
    all_to_all x1, waiting for transfers between devices, body(): moved = lax.all_to_all(tiles, FLUX_AXES, 0, 0, tiled=True)  11.3 us
    ppermute x1, waiting for transfers between devices, body(): far_part = lax.ppermute(sent, 'zh', ((0, 1), (1, 0)))  10 us
    all_to_all x1, starting transfers between devices, gather(): lax.all_to_all(jnp.broadcast_to(piece[None], (count, *piece.shape)), axes...  9.43 us
    pallas_call x1, Pallas kernels, basis(): pl.pallas_call(functools.partial(basis_kernel, root), out_shape=jax.Shape...  7.05 us
  transfers between devices with their start and end apart: 3, of which 3 were waited for; matrix products, arithmetic and copies ran while one was open for 1% of the time, Pallas kernels for 0%

profile of v1, /device:TPU:1, one launch (start us, length us, event | category | flops | bytes accessed | tf_op | source)
XLA Modules:
  0.0 134.5 jit_solution(14966519535669664640)
XLA Ops:
  0.6 2.5 %forward_tiles.1 = f32[32,8,128]{2,1,0:T(8,128)} custom-call(bf16[128,1024]{1,0:T(8,128)(2,1)} %far_jacobian.1, bf16[2,1024,128]{2,1,0:T(8,128)(2,1)} %far_probes.1, f32[8,128]{1,0:T(8,128)} %bitcast.18, f32[1,128]{1,0:T(1,128)} %bitcast.19), custom_call_target="tpu_custom_call" | custom-call | tf_op jit(solution)/shard_map/forward_tiles/pallas_call | solution.py:156
  3.1 15.9 %all-to-all-start = ((f32[32,8,128]{2,1,0:T(8,128)}), f32[32,8,128]{2,1,0:T(8,128)S(1)}, u32[]{:S(2)}, u32[]{:S(2)}) async-start(f32[32,8,128]{2,1,0:T(8,128)} %forward_tiles.1), calls=%async_computation | async-start | bytes 262144 | tf_op jit(solution)/shard_map/all_to_all | solution.py:207
  19.1 0.8 dynamic_slice.15
  19.8 0.0 copy-start.1
  19.8 11.3 %all-to-all-done = f32[32,8,128]{2,1,0:T(8,128)S(1)} async-done(((f32[32,8,128]{2,1,0:T(8,128)}), f32[32,8,128]{2,1,0:T(8,128)S(1)}, u32[]{:S(2)}, u32[]{:S(2)}) %all-to-all-start) | async-done | bytes 131104 | tf_op jit(solution)/shard_map/all_to_all | solution.py:207
  31.2 0.7 broadcast_in_dim.6
  31.9 9.4 %all-to-all-start.1 = ((bf16[64,8,128]{2,1,0:T(8,128)(2,1)}), bf16[64,8,128]{2,1,0:T(8,128)(2,1)S(1)}, u32[]{:S(2)}, u32[]{:S(2)}) async-start(bf16[64,8,128]{2,1,0:T(8,128)(2,1)} %broadcast_in_dim.6), calls=%async_computation.1 | async-start | bytes 262144 | tf_op jit(solution)/shard_map/all_to_all | solution.py:181
  41.3 0.0 copy-done.1
  41.4 11.7 %collective-permute-start = (bf16[128,512]{1,0:T(8,128)(2,1)S(1)}, bf16[128,512]{1,0:T(8,128)(2,1)S(1)}, u32[]{:S(2)}, u32[]{:S(2)}) collective-permute-start(bf16[128,512]{1,0:T(8,128)(2,1)S(1)} %constant_dynamic-slice_fusion), channel_id=1, source_target_pairs={{0,256},{256,0},{1,257},{257,1},{2,258},{258,2},{3,259},{259,3},{4... | collective-permute-start | bytes 393224 | tf_op jit(solution)/shard_map/ppermute | solution.py:205
  53.1 3.2 %all-to-all-done.1 = bf16[64,8,128]{2,1,0:T(8,128)(2,1)S(1)} async-done(((bf16[64,8,128]{2,1,0:T(8,128)(2,1)}), bf16[64,8,128]{2,1,0:T(8,128)(2,1)S(1)}, u32[]{:S(2)}, u32[]{:S(2)}) %all-to-all-start.1) | async-done | bytes 131104 | tf_op jit(solution)/shard_map/all_to_all | solution.py:181
  56.3 0.3 fusion.2
  56.6 10.0 %collective-permute-done = bf16[128,512]{1,0:T(8,128)(2,1)S(1)} collective-permute-done((bf16[128,512]{1,0:T(8,128)(2,1)S(1)}, bf16[128,512]{1,0:T(8,128)(2,1)S(1)}, u32[]{:S(2)}, u32[]{:S(2)}) %collective-permute-start) | collective-permute-done | bytes 131104 | tf_op jit(solution)/shard_map/ppermute | solution.py:205
  66.7 0.2 fusion
  66.9 12.6 %all_to_all.30 = bf16[8,64,256]{2,1,0:T(8,128)(2,1)S(1)} all-to-all(bf16[8,64,256]{2,1,0:T(8,128)(2,1)S(1)} %bitcast.15), channel_id=1, replica_groups=mesh['zh'=2,'y'=4,'c'=2,'zl'=8,'x'=4] {'y','c'}, dimensions={0} | all-to-all | bytes 524288 | tf_op jit(solution)/shard_map/all_to_all | solution.py:175
  79.6 0.1 broadcast_multiply_fusion.sketch
  79.7 0.0 copy-start
  79.7 0.4 fusion.1
  80.1 13.3 %all_to_all.31 = bf16[32,8,256]{2,1,0:T(8,128)(2,1)S(1)} all-to-all(bf16[32,8,256]{2,1,0:T(8,128)(2,1)S(1)} %fusion.1), channel_id=1, replica_groups=mesh['zh'=2,'y'=4,'c'=2,'zl'=8,'x'=4] {'y','c','x'}, dimensions={0} | all-to-all | bytes 262144 | tf_op jit(solution)/shard_map/all_to_all | solution.py:175
  93.4 19.7 %all_to_all.32 = bf16[16,8,256]{2,1,0:T(8,128)(2,1)S(1)} all-to-all(bf16[16,8,256]{2,1,0:T(8,128)(2,1)S(1)} %broadcast_in_dim.7), channel_id=1, replica_groups=mesh['zh'=2,'y'=4,'c'=2,'zl'=8,'x'=4] {'zh','zl'}, dimensions={0} | all-to-all | bytes 131072 | tf_op jit(solution)/shard_map/all_to_all | solution.py:181
  113.2 14.2 %all_to_all.33 = f32[32,8,256]{2,1,0:T(8,128)S(1)} all-to-all(f32[32,8,256]{2,1,0:T(8,128)S(1)} %broadcast_in_dim.8), channel_id=1, replica_groups=mesh['zh'=2,'y'=4,'c'=2,'zl'=8,'x'=4] {'y','c','x'}, dimensions={0} | all-to-all | bytes 524288 | tf_op jit(solution)/shard_map/all_to_all | solution.py:181
  127.4 0.0 copy-done
  127.4 7.0 %cholesky_basis.1 = f32[64,256]{1,0:T(8,128)} custom-call(f32[256,256]{1,0:T(8,128)S(1)} %bitcast.14, f32[64,256]{1,0:T(8,128)S(1)} %broadcast_multiply_fusion.sketch), custom_call_target="tpu_custom_call" | custom-call | tf_op jit(solution)/shard_map/cholesky_basis/pallas_call | solution.py:104
  (7 shorter events, 0.2 us)
Async XLA Ops:
  3.1 28.1 %all-to-all-start = ((f32[32,8,128]{2,1,0:T(8,128)}), f32[32,8,128]{2,1,0:T(8,128)S(1)}, u32[]{:S(2)}, u32[]{:S(2)}) async-start(f32[32,8,128]{2,1,0:T(8,128)} %forward_tiles.1), calls=%async_computation | async-start | bytes 262144 | tf_op jit(solution)/shard_map/all_to_all | solution.py:207
  19.8 21.5 %copy-start.1 = (bf16[128,1024]{1,0:T(8,128)(2,1)S(1)}, bf16[128,1024]{1,0:T(8,128)(2,1)}, u32[]{:S(2)}) copy-start(bf16[128,1024]{1,0:T(8,128)(2,1)} %far_jacobian.1) | copy-start | bytes 786436
  31.9 24.4 %all-to-all-start.1 = ((bf16[64,8,128]{2,1,0:T(8,128)(2,1)}), bf16[64,8,128]{2,1,0:T(8,128)(2,1)S(1)}, u32[]{:S(2)}, u32[]{:S(2)}) async-start(bf16[64,8,128]{2,1,0:T(8,128)(2,1)} %broadcast_in_dim.6), calls=%async_computation.1 | async-start | bytes 262144 | tf_op jit(solution)/shard_map/all_to_all | solution.py:181
  41.4 25.3 %collective-permute-start = (bf16[128,512]{1,0:T(8,128)(2,1)S(1)}, bf16[128,512]{1,0:T(8,128)(2,1)S(1)}, u32[]{:S(2)}, u32[]{:S(2)}) collective-permute-start(bf16[128,512]{1,0:T(8,128)(2,1)S(1)} %constant_dynamic-slice_fusion), channel_id=1, source_target_pairs={{0,256},{256,0},{1,257},{257,1},{2,258},{258,2},{3,259},{259,3},{4... | collective-permute-start | bytes 393224 | tf_op jit(solution)/shard_map/ppermute | solution.py:205
  79.7 47.7 %copy-start = (f32[64,256]{1,0:T(8,128)}, f32[64,256]{1,0:T(8,128)S(1)}, u32[]{:S(2)}) copy-start(f32[64,256]{1,0:T(8,128)S(1)} %broadcast_multiply_fusion.sketch) | copy-start | bytes 196612

commit v2 on v1

--- a/solution.py
+++ b/solution.py
@@ -15,7 +15,6 @@
 LINE = ("zh", "zl")
 HALF = 128
 STEP = 8
-CHUNKS = 4
 VMEM_LIMIT = 16 * 2**20
 HIGHEST = lax.Precision.HIGHEST
 
@@ -83,12 +82,15 @@
     return lax.dot_general(a, b, (dims, ((), ())), precision=HIGHEST, preferred_element_type=jnp.float32)
 
 
-def basis_kernel(root, gram, sketch, out, diag, low, high, lanes, near):
-    diag[...] = gram[:HALF, :HALF]
+def basis_kernel(root, packed, sketch, out, gram, diag, low, high, lanes, near):
+    rows = packed.shape[1]
+    for k in range(packed.shape[0]):
+        gram[k * rows : (k + 1) * rows, :] = packed[k]
+    diag[...] = gram[:, :HALF]
     low[...] = identity()
     eliminate(diag, low, lanes, near)
-    upper = dot(low[...], gram[:HALF, HALF:], ((1,), (0,)))
-    diag[...] = gram[HALF:, HALF:] - dot(upper, upper, ((0,), (0,)))
+    upper = dot(low[...], gram[:, HALF : 2 * HALF], ((1,), (0,)))
+    diag[...] = gram[:, 2 * HALF :] - dot(upper, upper, ((0,), (0,)))
     high[...] = identity()
     eliminate(diag, high, lanes, near)
     first, second = sketch[:, :HALF], sketch[:, HALF:]
@@ -106,43 +108,37 @@
         out_shape=jax.ShapeDtypeStruct(sketch.shape, jnp.float32),
         in_specs=[vmem, vmem],
         out_specs=vmem,
-        scratch_shapes=[square, square, square, *[pltpu.VMEM((2 * STEP * STEP, HALF), jnp.float32)] * 2],
+        scratch_shapes=[pltpu.VMEM((HALF, 3 * HALF), jnp.float32), square, square, square, *[pltpu.VMEM((2 * STEP * STEP, HALF), jnp.float32)] * 2],
         compiler_params=pltpu.CompilerParams(vmem_limit_bytes=VMEM_LIMIT),
         name="cholesky_basis",
     )(gram, sketch)
 
 
 def forward_kernel(
-    far_jacobian, far_probes, far_spread, far_weight, far_out, jacobian, probes, spread, weight, stacked, out, sems
+    far_jacobian, far_probes, far_spread, far_weight, far_out, jacobian, probes, spread, weight, out, sems
 ):
     sub = lax.broadcasted_iota(jnp.int32, (STEP, HALF), 0)
     blocks, flux_local, _ = probes.shape
-    pair, chunk = 2 * STEP, flux_local // CHUNKS
-    copies = [pltpu.make_async_copy(far_spread, spread, sems.at[CHUNKS])]
-    for c in range(CHUNKS):
-        part = (slice(None), pl.ds(c * chunk, chunk), slice(None))
-        copies.append(pltpu.make_async_copy(far_probes.at[part], probes.at[part], sems.at[c]))
-    copies.append(pltpu.make_async_copy(far_weight, weight, sems.at[CHUNKS + 2]))
-    copies.append(pltpu.make_async_copy(far_jacobian, jacobian, sems.at[CHUNKS + 1]))
+    pair = 2 * STEP
+    pairs = ((far_spread, spread), (far_probes, probes), (far_jacobian, jacobian), (far_weight, weight))
+    copies = [pltpu.make_async_copy(*ends, sems.at[i]) for i, ends in enumerate(pairs)]
     for copy in copies:
         copy.start()
-    copies[0].wait()
+    for copy in copies:
+        copy.wait()
+    stacked = []
     for low in range(0, flux_local, pair):
-        if low % chunk == 0:
-            copies[1 + low // chunk].wait()
         row = spread[pl.ds(low // HALF, STEP, stride=0), :]
         factor = jnp.concatenate([pick(row, sub + (low + half) % HALF) for half in (0, STEP)], axis=0)
-        for b in range(blocks):
-            scaled = probes[b, low : low + pair, :].astype(jnp.float32) * factor
-            stacked[low : low + pair, b * HALF : (b + 1) * HALF] = scaled.astype(jnp.bfloat16)
-    copies[-2].wait()
+        scaled = [probes[b, low : low + pair, :].astype(jnp.float32) * factor for b in range(blocks)]
+        stacked.append(jnp.concatenate([block.astype(jnp.bfloat16) for block in scaled], axis=1))
+    stacked = jnp.concatenate(stacked, axis=0)
     row = weight[pl.ds(0, STEP, stride=0), :]
-    copies[-1].wait()
-    total = jnp.dot(jacobian[...], stacked[...], preferred_element_type=jnp.float32)
+    total = jnp.dot(jacobian[...], stacked, preferred_element_type=jnp.float32)
     for k in range(out.shape[0]):
         r, c = k // blocks * STEP, k % blocks * HALF
         out[k] = total[r : r + STEP, c : c + HALF] * pick(row, sub + r)
-    result = pltpu.make_async_copy(out, far_out, sems.at[CHUNKS])
+    result = pltpu.make_async_copy(out, far_out, sems.at[0])
     result.start()
     result.wait()
 
@@ -163,9 +159,8 @@
             pltpu.VMEM(probes.shape, probes.dtype),
             pltpu.VMEM(spread.shape, spread.dtype),
             pltpu.VMEM((1, rows), jnp.float32),
-            pltpu.VMEM((flux_local, columns), jnp.bfloat16),
             pltpu.VMEM(shape, jnp.float32),
-            pltpu.SemaphoreType.DMA((CHUNKS + 3,)),
+            pltpu.SemaphoreType.DMA((4,)),
         ],
         name="forward_tiles",
     )(jacobian, probes, spread, obs_weight.reshape(1, rows))
@@ -214,13 +209,14 @@
     adjoint += pull(far_part, lax.dynamic_slice_in_dim(weighted, rows[1], obs_local))
     adjoint = scatter_sum(adjoint.astype(jnp.bfloat16).reshape(-1, portion, columns), NEAR_OBS)
     sketch = adjoint * local_std[:, None]
-    gram = jnp.dot(
-        sketch.T, sketch, precision=lax.Precision.HIGHEST, preferred_element_type=jnp.float32
+    left, right = sketch[:, :HALF], sketch[:, HALF:]
+    gram = jnp.concatenate(
+        [dot(left, sketch, ((0,), (0,))), dot(right, right, ((0,), (0,)))], axis=1
     )
-    slab = scatter_sum(gram.astype(jnp.bfloat16).reshape(lax.axis_size(PLANE), -1, columns), PLANE)
-    slab = lax.optimization_barrier(slab).astype(jnp.bfloat16)
+    slab = gram.astype(jnp.bfloat16).reshape(lax.axis_size(PLANE), -1, gram.shape[1])
+    slab = lax.optimization_barrier(scatter_sum(slab, PLANE)).astype(jnp.bfloat16)
     slab = jnp.sum(gather(slab, LINE).astype(jnp.float32), axis=0)
-    gram = gather(slab, PLANE).reshape(columns, columns)
+    gram = gather(slab, PLANE)
     scale_root = math.sqrt(flux_local * lax.axis_size(FLUX_AXES))
     return (sketch, basis(gram, sketch, scale_root))
 

time: 135 us -> 134 us (level)
  no operation moved by 1% of the time
where the time goes in v2:
time: 134 us
  blocking collectives  58.7 us (44%)
  starting transfers between devices  37.1 us (28%)
  waiting for transfers between devices  24.6 us (18%)
  Pallas kernels  9.43 us (7%)
  local copies, waits for them, and re-layouts  1.52 us (1%)
    all_to_all x2, blocking collectives, gather(): lax.all_to_all(jnp.broadcast_to(piece[None], (count, *piece.shape)), axes...  33.1 us
    all_to_all x2, blocking collectives, scatter_sum(): moved = lax.all_to_all(parts, axes, 0, 0, tiled=True)  25.6 us
    all_to_all x1, starting transfers between devices, body(): moved = lax.all_to_all(tiles, FLUX_AXES, 0, 0, tiled=True)  15.9 us
    ppermute x1, starting transfers between devices, body(): far_part = lax.ppermute(sent, 'zh', ((0, 1), (1, 0)))  11.7 us
    all_to_all x1, waiting for transfers between devices, body(): moved = lax.all_to_all(tiles, FLUX_AXES, 0, 0, tiled=True)  11.3 us
    ppermute x1, waiting for transfers between devices, body(): far_part = lax.ppermute(sent, 'zh', ((0, 1), (1, 0)))  10 us
    all_to_all x1, starting transfers between devices, gather(): lax.all_to_all(jnp.broadcast_to(piece[None], (count, *piece.shape)), axes...  9.43 us
    pallas_call x1, Pallas kernels, basis(): pl.pallas_call(functools.partial(basis_kernel, root), out_shape=jax.Shape...  7.06 us
  transfers between devices with their start and end apart: 3, of which 3 were waited for; matrix products, arithmetic and copies ran while one was open for 1% of the time, Pallas kernels for 0%

profile of v2, /device:TPU:1, one launch (start us, length us, event | category | flops | bytes accessed | tf_op | source)
XLA Modules:
  0.0 133.6 jit_solution(14167447289960301320)
XLA Ops:
  0.6 2.4 %forward_tiles.1 = f32[32,8,128]{2,1,0:T(8,128)} custom-call(bf16[128,1024]{1,0:T(8,128)(2,1)} %far_jacobian.1, bf16[2,1024,128]{2,1,0:T(8,128)(2,1)} %far_probes.1, f32[8,128]{1,0:T(8,128)} %bitcast.15, f32[1,128]{1,0:T(1,128)} %bitcast.16), custom_call_target="tpu_custom_call" | custom-call | tf_op jit(solution)/shard_map/forward_tiles/pallas_call | solution.py:152
  3.0 15.9 %all-to-all-start = ((f32[32,8,128]{2,1,0:T(8,128)}), f32[32,8,128]{2,1,0:T(8,128)S(1)}, u32[]{:S(2)}, u32[]{:S(2)}) async-start(f32[32,8,128]{2,1,0:T(8,128)} %forward_tiles.1), calls=%async_computation | async-start | bytes 262144 | tf_op jit(solution)/shard_map/all_to_all | solution.py:202
  18.9 0.8 dynamic_slice.15
  19.7 0.0 copy-start.1
  19.7 11.3 %all-to-all-done = f32[32,8,128]{2,1,0:T(8,128)S(1)} async-done(((f32[32,8,128]{2,1,0:T(8,128)}), f32[32,8,128]{2,1,0:T(8,128)S(1)}, u32[]{:S(2)}, u32[]{:S(2)}) %all-to-all-start) | async-done | bytes 131104 | tf_op jit(solution)/shard_map/all_to_all | solution.py:202
  31.1 0.7 broadcast_in_dim.6
  31.8 9.4 %all-to-all-start.1 = ((bf16[64,8,128]{2,1,0:T(8,128)(2,1)}), bf16[64,8,128]{2,1,0:T(8,128)(2,1)S(1)}, u32[]{:S(2)}, u32[]{:S(2)}) async-start(bf16[64,8,128]{2,1,0:T(8,128)(2,1)} %broadcast_in_dim.6), calls=%async_computation.1 | async-start | bytes 262144 | tf_op jit(solution)/shard_map/all_to_all | solution.py:176
  41.2 0.0 copy-done.1
  41.2 11.7 %collective-permute-start = (bf16[128,512]{1,0:T(8,128)(2,1)S(1)}, bf16[128,512]{1,0:T(8,128)(2,1)S(1)}, u32[]{:S(2)}, u32[]{:S(2)}) collective-permute-start(bf16[128,512]{1,0:T(8,128)(2,1)S(1)} %constant_dynamic-slice_fusion), channel_id=1, source_target_pairs={{0,256},{256,0},{1,257},{257,1},{2,258},{258,2},{3,259},{259,3},{4... | collective-permute-start | bytes 393224 | tf_op jit(solution)/shard_map/ppermute | solution.py:200
  53.0 3.2 %all-to-all-done.1 = bf16[64,8,128]{2,1,0:T(8,128)(2,1)S(1)} async-done(((bf16[64,8,128]{2,1,0:T(8,128)(2,1)}), bf16[64,8,128]{2,1,0:T(8,128)(2,1)S(1)}, u32[]{:S(2)}, u32[]{:S(2)}) %all-to-all-start.1) | async-done | bytes 131104 | tf_op jit(solution)/shard_map/all_to_all | solution.py:176
  56.2 0.3 fusion.1
  56.5 10.0 %collective-permute-done = bf16[128,512]{1,0:T(8,128)(2,1)S(1)} collective-permute-done((bf16[128,512]{1,0:T(8,128)(2,1)S(1)}, bf16[128,512]{1,0:T(8,128)(2,1)S(1)}, u32[]{:S(2)}, u32[]{:S(2)}) %collective-permute-start) | collective-permute-done | bytes 131104 | tf_op jit(solution)/shard_map/ppermute | solution.py:200
  66.6 0.3 fusion
  66.8 12.6 %all_to_all.30 = bf16[8,64,256]{2,1,0:T(8,128)(2,1)S(1)} all-to-all(bf16[8,64,256]{2,1,0:T(8,128)(2,1)S(1)} %bitcast.11), channel_id=1, replica_groups=mesh['zh'=2,'y'=4,'c'=2,'zl'=8,'x'=4] {'y','c'}, dimensions={0} | all-to-all | bytes 524288 | tf_op jit(solution)/shard_map/all_to_all | solution.py:170
  79.5 0.1 broadcast_multiply_fusion.sketch
  79.6 0.0 copy-start
  79.6 0.3 convolution_convert_fusion.1
  79.9 0.3 convolution_convert_fusion
  80.3 13.0 %all_to_all.31 = bf16[32,4,384]{2,1,0:T(4,128)(2,1)S(1)} all-to-all(bf16[32,4,384]{2,1,0:T(4,128)(2,1)S(1)} %pad_maximum_fusion), channel_id=1, replica_groups=mesh['zh'=2,'y'=4,'c'=2,'zl'=8,'x'=4] {'y','c','x'}, dimensions={0} | all-to-all | bytes 196608 | tf_op jit(solution)/shard_map/all_to_all | solution.py:170
  93.2 0.1 convert_reduce_fusion.1
  93.3 19.7 %all_to_all.32 = bf16[16,4,384]{2,1,0:T(4,128)(2,1)S(1)} all-to-all(bf16[16,4,384]{2,1,0:T(4,128)(2,1)S(1)} %broadcast_in_dim.7), channel_id=1, replica_groups=mesh['zh'=2,'y'=4,'c'=2,'zl'=8,'x'=4] {'zh','zl'}, dimensions={0} | all-to-all | bytes 98304 | tf_op jit(solution)/shard_map/all_to_all | solution.py:176
  113.1 13.4 %all_to_all.33.packed = f32[32,4,384]{2,1,0:T(4,128)S(1)} all-to-all(f32[32,4,384]{2,1,0:T(4,128)S(1)} %broadcast_in_dim.8), channel_id=1, replica_groups=mesh['zh'=2,'y'=4,'c'=2,'zl'=8,'x'=4] {'y','c','x'}, dimensions={0} | all-to-all | bytes 393216 | tf_op jit(solution)/shard_map/all_to_all | solution.py:176
  126.5 0.0 copy-done
  126.5 7.1 %cholesky_basis.1 = f32[64,256]{1,0:T(8,128)} custom-call(f32[32,4,384]{2,1,0:T(4,128)S(1)} %all_to_all.33.packed, f32[64,256]{1,0:T(8,128)S(1)} %broadcast_multiply_fusion.sketch), custom_call_target="tpu_custom_call" | custom-call | tf_op jit(solution)/shard_map/cholesky_basis/pallas_call | solution.py:106
  (8 shorter events, 0.2 us)
Async XLA Ops:
  3.0 28.1 %all-to-all-start = ((f32[32,8,128]{2,1,0:T(8,128)}), f32[32,8,128]{2,1,0:T(8,128)S(1)}, u32[]{:S(2)}, u32[]{:S(2)}) async-start(f32[32,8,128]{2,1,0:T(8,128)} %forward_tiles.1), calls=%async_computation | async-start | bytes 262144 | tf_op jit(solution)/shard_map/all_to_all | solution.py:202
  19.7 21.5 %copy-start.1 = (bf16[128,1024]{1,0:T(8,128)(2,1)S(1)}, bf16[128,1024]{1,0:T(8,128)(2,1)}, u32[]{:S(2)}) copy-start(bf16[128,1024]{1,0:T(8,128)(2,1)} %far_jacobian.1) | copy-start | bytes 786436
  31.8 24.4 %all-to-all-start.1 = ((bf16[64,8,128]{2,1,0:T(8,128)(2,1)}), bf16[64,8,128]{2,1,0:T(8,128)(2,1)S(1)}, u32[]{:S(2)}, u32[]{:S(2)}) async-start(bf16[64,8,128]{2,1,0:T(8,128)(2,1)} %broadcast_in_dim.6), calls=%async_computation.1 | async-start | bytes 262144 | tf_op jit(solution)/shard_map/all_to_all | solution.py:176
  41.2 25.3 %collective-permute-start = (bf16[128,512]{1,0:T(8,128)(2,1)S(1)}, bf16[128,512]{1,0:T(8,128)(2,1)S(1)}, u32[]{:S(2)}, u32[]{:S(2)}) collective-permute-start(bf16[128,512]{1,0:T(8,128)(2,1)S(1)} %constant_dynamic-slice_fusion), channel_id=1, source_target_pairs={{0,256},{256,0},{1,257},{257,1},{2,258},{258,2},{3,259},{259,3},{4... | collective-permute-start | bytes 393224 | tf_op jit(solution)/shard_map/ppermute | solution.py:200
  79.6 47.0 %copy-start = (f32[64,256]{1,0:T(8,128)}, f32[64,256]{1,0:T(8,128)S(1)}, u32[]{:S(2)}) copy-start(f32[64,256]{1,0:T(8,128)S(1)} %broadcast_multiply_fusion.sketch) | copy-start | bytes 196612

commit v3 on v2

--- a/solution.py
+++ b/solution.py
@@ -209,10 +209,11 @@
     adjoint += pull(far_part, lax.dynamic_slice_in_dim(weighted, rows[1], obs_local))
     adjoint = scatter_sum(adjoint.astype(jnp.bfloat16).reshape(-1, portion, columns), NEAR_OBS)
     sketch = adjoint * local_std[:, None]
-    left, right = sketch[:, :HALF], sketch[:, HALF:]
-    gram = jnp.concatenate(
-        [dot(left, sketch, ((0,), (0,))), dot(right, right, ((0,), (0,)))], axis=1
+    gram = lax.dot_general(
+        sketch, sketch, (((0,), (0,)), ((), ())),
+        precision=lax.Precision.HIGH, preferred_element_type=jnp.float32,
     )
+    gram = jnp.concatenate([gram[:HALF], gram[HALF:, HALF:]], axis=1)
     slab = gram.astype(jnp.bfloat16).reshape(lax.axis_size(PLANE), -1, gram.shape[1])
     slab = lax.optimization_barrier(scatter_sum(slab, PLANE)).astype(jnp.bfloat16)
     slab = jnp.sum(gather(slab, LINE).astype(jnp.float32), axis=0)

time: 134 us -> 134 us (level)
  no operation moved by 1% of the time
where the time goes in v3:
time: 134 us; the launch traced here: 133 us
  blocking collectives  58.7 us (44%)
  starting transfers between devices  37.1 us (28%)
  waiting for transfers between devices  24.6 us (18%)
  Pallas kernels  9.43 us (7%)
  local copies, waits for them, and re-layouts  1.53 us (1%)
    all_to_all x2, blocking collectives, gather(): lax.all_to_all(jnp.broadcast_to(piece[None], (count, *piece.shape)), axes...  33.1 us
    all_to_all x2, blocking collectives, scatter_sum(): moved = lax.all_to_all(parts, axes, 0, 0, tiled=True)  25.6 us
    all_to_all x1, starting transfers between devices, body(): moved = lax.all_to_all(tiles, FLUX_AXES, 0, 0, tiled=True)  15.9 us
    ppermute x1, starting transfers between devices, body(): far_part = lax.ppermute(sent, 'zh', ((0, 1), (1, 0)))  11.7 us
    all_to_all x1, waiting for transfers between devices, body(): moved = lax.all_to_all(tiles, FLUX_AXES, 0, 0, tiled=True)  11.3 us
    ppermute x1, waiting for transfers between devices, body(): far_part = lax.ppermute(sent, 'zh', ((0, 1), (1, 0)))  10 us
    all_to_all x1, starting transfers between devices, gather(): lax.all_to_all(jnp.broadcast_to(piece[None], (count, *piece.shape)), axes...  9.43 us
    pallas_call x1, Pallas kernels, basis(): pl.pallas_call(functools.partial(basis_kernel, root), out_shape=jax.Shape...  7.06 us
  transfers between devices with their start and end apart: 3, of which 3 were waited for; matrix products, arithmetic and copies ran while one was open for 1% of the time, Pallas kernels for 0%

profile of v3, /device:TPU:1, one launch (start us, length us, event | category | flops | bytes accessed | tf_op | source)
XLA Modules:
  0.0 133.3 jit_solution(2896830211434279082)
XLA Ops:
  0.6 2.4 %forward_tiles.1 = f32[32,8,128]{2,1,0:T(8,128)} custom-call(bf16[128,1024]{1,0:T(8,128)(2,1)} %far_jacobian.1, bf16[2,1024,128]{2,1,0:T(8,128)(2,1)} %far_probes.1, f32[8,128]{1,0:T(8,128)} %bitcast.16, f32[1,128]{1,0:T(1,128)} %bitcast.17), custom_call_target="tpu_custom_call" | custom-call | tf_op jit(solution)/shard_map/forward_tiles/pallas_call | solution.py:152
  3.0 15.9 %all-to-all-start = ((f32[32,8,128]{2,1,0:T(8,128)}), f32[32,8,128]{2,1,0:T(8,128)S(1)}, u32[]{:S(2)}, u32[]{:S(2)}) async-start(f32[32,8,128]{2,1,0:T(8,128)} %forward_tiles.1), calls=%async_computation | async-start | bytes 262144 | tf_op jit(solution)/shard_map/all_to_all | solution.py:202
  18.9 0.8 dynamic_slice.15
  19.7 0.0 copy-start.1
  19.7 11.3 %all-to-all-done = f32[32,8,128]{2,1,0:T(8,128)S(1)} async-done(((f32[32,8,128]{2,1,0:T(8,128)}), f32[32,8,128]{2,1,0:T(8,128)S(1)}, u32[]{:S(2)}, u32[]{:S(2)}) %all-to-all-start) | async-done | bytes 131104 | tf_op jit(solution)/shard_map/all_to_all | solution.py:202
  31.1 0.7 broadcast_in_dim.6
  31.8 9.4 %all-to-all-start.1 = ((bf16[64,8,128]{2,1,0:T(8,128)(2,1)}), bf16[64,8,128]{2,1,0:T(8,128)(2,1)S(1)}, u32[]{:S(2)}, u32[]{:S(2)}) async-start(bf16[64,8,128]{2,1,0:T(8,128)(2,1)} %broadcast_in_dim.6), calls=%async_computation.1 | async-start | bytes 262144 | tf_op jit(solution)/shard_map/all_to_all | solution.py:176
  41.2 0.0 copy-done.1
  41.2 11.7 %collective-permute-start = (bf16[128,512]{1,0:T(8,128)(2,1)S(1)}, bf16[128,512]{1,0:T(8,128)(2,1)S(1)}, u32[]{:S(2)}, u32[]{:S(2)}) collective-permute-start(bf16[128,512]{1,0:T(8,128)(2,1)S(1)} %constant_dynamic-slice_fusion), channel_id=1, source_target_pairs={{0,256},{256,0},{1,257},{257,1},{2,258},{258,2},{3,259},{259,3},{4... | collective-permute-start | bytes 393224 | tf_op jit(solution)/shard_map/ppermute | solution.py:200
  53.0 3.2 %all-to-all-done.1 = bf16[64,8,128]{2,1,0:T(8,128)(2,1)S(1)} async-done(((bf16[64,8,128]{2,1,0:T(8,128)(2,1)}), bf16[64,8,128]{2,1,0:T(8,128)(2,1)S(1)}, u32[]{:S(2)}, u32[]{:S(2)}) %all-to-all-start.1) | async-done | bytes 131104 | tf_op jit(solution)/shard_map/all_to_all | solution.py:176
  56.2 0.3 fusion.1
  56.5 10.0 %collective-permute-done = bf16[128,512]{1,0:T(8,128)(2,1)S(1)} collective-permute-done((bf16[128,512]{1,0:T(8,128)(2,1)S(1)}, bf16[128,512]{1,0:T(8,128)(2,1)S(1)}, u32[]{:S(2)}, u32[]{:S(2)}) %collective-permute-start) | collective-permute-done | bytes 131104 | tf_op jit(solution)/shard_map/ppermute | solution.py:200
  66.6 0.3 fusion
  66.8 12.6 %all_to_all.30 = bf16[8,64,256]{2,1,0:T(8,128)(2,1)S(1)} all-to-all(bf16[8,64,256]{2,1,0:T(8,128)(2,1)S(1)} %bitcast.12), channel_id=1, replica_groups=mesh['zh'=2,'y'=4,'c'=2,'zl'=8,'x'=4] {'y','c'}, dimensions={0} | all-to-all | bytes 524288 | tf_op jit(solution)/shard_map/all_to_all | solution.py:170
  79.5 0.1 broadcast_multiply_fusion.sketch
  79.6 0.0 copy-start
  79.6 0.3 convolution_convert_fusion
  80.0 13.0 %all_to_all.31 = bf16[32,4,384]{2,1,0:T(4,128)(2,1)S(1)} all-to-all(bf16[32,4,384]{2,1,0:T(4,128)(2,1)S(1)} %pad_maximum_fusion), channel_id=1, replica_groups=mesh['zh'=2,'y'=4,'c'=2,'zl'=8,'x'=4] {'y','c','x'}, dimensions={0} | all-to-all | bytes 196608 | tf_op jit(solution)/shard_map/all_to_all | solution.py:170
  93.0 0.1 convert_reduce_fusion.1
  93.1 19.7 %all_to_all.32 = bf16[16,4,384]{2,1,0:T(4,128)(2,1)S(1)} all-to-all(bf16[16,4,384]{2,1,0:T(4,128)(2,1)S(1)} %broadcast_in_dim.7), channel_id=1, replica_groups=mesh['zh'=2,'y'=4,'c'=2,'zl'=8,'x'=4] {'zh','zl'}, dimensions={0} | all-to-all | bytes 98304 | tf_op jit(solution)/shard_map/all_to_all | solution.py:176
  112.8 13.4 %all_to_all.33.packed = f32[32,4,384]{2,1,0:T(4,128)S(1)} all-to-all(f32[32,4,384]{2,1,0:T(4,128)S(1)} %broadcast_in_dim.8), channel_id=1, replica_groups=mesh['zh'=2,'y'=4,'c'=2,'zl'=8,'x'=4] {'y','c','x'}, dimensions={0} | all-to-all | bytes 393216 | tf_op jit(solution)/shard_map/all_to_all | solution.py:176
  126.2 0.0 copy-done
  126.2 7.1 %cholesky_basis.1 = f32[64,256]{1,0:T(8,128)} custom-call(f32[32,4,384]{2,1,0:T(4,128)S(1)} %all_to_all.33.packed, f32[64,256]{1,0:T(8,128)S(1)} %broadcast_multiply_fusion.sketch), custom_call_target="tpu_custom_call" | custom-call | tf_op jit(solution)/shard_map/cholesky_basis/pallas_call | solution.py:106
  (10 shorter events, 0.2 us)
Async XLA Ops:
  3.0 28.1 %all-to-all-start = ((f32[32,8,128]{2,1,0:T(8,128)}), f32[32,8,128]{2,1,0:T(8,128)S(1)}, u32[]{:S(2)}, u32[]{:S(2)}) async-start(f32[32,8,128]{2,1,0:T(8,128)} %forward_tiles.1), calls=%async_computation | async-start | bytes 262144 | tf_op jit(solution)/shard_map/all_to_all | solution.py:202
  19.7 21.5 %copy-start.1 = (bf16[128,1024]{1,0:T(8,128)(2,1)S(1)}, bf16[128,1024]{1,0:T(8,128)(2,1)}, u32[]{:S(2)}) copy-start(bf16[128,1024]{1,0:T(8,128)(2,1)} %far_jacobian.1) | copy-start | bytes 786436
  31.8 24.4 %all-to-all-start.1 = ((bf16[64,8,128]{2,1,0:T(8,128)(2,1)}), bf16[64,8,128]{2,1,0:T(8,128)(2,1)S(1)}, u32[]{:S(2)}, u32[]{:S(2)}) async-start(bf16[64,8,128]{2,1,0:T(8,128)(2,1)} %broadcast_in_dim.6), calls=%async_computation.1 | async-start | bytes 262144 | tf_op jit(solution)/shard_map/all_to_all | solution.py:176
  41.2 25.3 %collective-permute-start = (bf16[128,512]{1,0:T(8,128)(2,1)S(1)}, bf16[128,512]{1,0:T(8,128)(2,1)S(1)}, u32[]{:S(2)}, u32[]{:S(2)}) collective-permute-start(bf16[128,512]{1,0:T(8,128)(2,1)S(1)} %constant_dynamic-slice_fusion), channel_id=1, source_target_pairs={{0,256},{256,0},{1,257},{257,1},{2,258},{258,2},{3,259},{259,3},{4... | collective-permute-start | bytes 393224 | tf_op jit(solution)/shard_map/ppermute | solution.py:200
  79.6 46.7 %copy-start = (f32[64,256]{1,0:T(8,128)}, f32[64,256]{1,0:T(8,128)S(1)}, u32[]{:S(2)}) copy-start(f32[64,256]{1,0:T(8,128)S(1)} %broadcast_multiply_fusion.sketch) | copy-start | bytes 196612

commit v4 on v3

--- a/solution.py
+++ b/solution.py
@@ -201,12 +201,12 @@
     tiles = forward_tiles(jacobian, probes, prior_std, obs_weight)
     moved = lax.all_to_all(tiles, FLUX_AXES, 0, 0, tiled=True)
     tile = jnp.sum(moved, axis=0)
-    tile, local_std, rows = lax.optimization_barrier((tile, local_std, rows))
     near_part = lax.dynamic_slice_in_dim(jacobian, rows[2], half, 1)
+    tile, local_std, rows, near_part = lax.optimization_barrier((tile, local_std, rows, near_part))
     weighted = gather(tile.astype(jnp.bfloat16), ("zh",) + FLUX_AXES)
     weighted = from_tiles(weighted, 2 * obs_local, columns)
-    adjoint = pull(near_part, lax.dynamic_slice_in_dim(weighted, rows[0], obs_local))
-    adjoint += pull(far_part, lax.dynamic_slice_in_dim(weighted, rows[1], obs_local))
+    parts = [lax.dynamic_slice_in_dim(weighted, row, obs_local) for row in rows[:2]]
+    adjoint = pull(jnp.concatenate([near_part, far_part]), jnp.concatenate(parts))
     adjoint = scatter_sum(adjoint.astype(jnp.bfloat16).reshape(-1, portion, columns), NEAR_OBS)
     sketch = adjoint * local_std[:, None]
     gram = lax.dot_general(

time: 134 us -> 134 us (level)
  no operation moved by 1% of the time
where the time goes in v4:
time: 134 us; the launch traced here: 133 us
  blocking collectives  58.6 us (44%)
  starting transfers between devices  37.2 us (28%)
  waiting for transfers between devices  24.9 us (19%)
  Pallas kernels  9.43 us (7%)
  local copies, waits for them, and re-layouts  1.57 us (1%)
    all_to_all x2, blocking collectives, gather(): lax.all_to_all(jnp.broadcast_to(piece[None], (count, *piece.shape)), axes...  33.1 us
    all_to_all x2, blocking collectives, scatter_sum(): moved = lax.all_to_all(parts, axes, 0, 0, tiled=True)  25.6 us
    all_to_all x1, starting transfers between devices, body(): moved = lax.all_to_all(tiles, FLUX_AXES, 0, 0, tiled=True)  16.1 us
    ppermute x1, starting transfers between devices, body(): far_part = lax.ppermute(sent, 'zh', ((0, 1), (1, 0)))  11.7 us
    all_to_all x1, waiting for transfers between devices, body(): moved = lax.all_to_all(tiles, FLUX_AXES, 0, 0, tiled=True)  11.3 us
    ppermute x1, waiting for transfers between devices, body(): far_part = lax.ppermute(sent, 'zh', ((0, 1), (1, 0)))  10.4 us
    all_to_all x1, starting transfers between devices, gather(): lax.all_to_all(jnp.broadcast_to(piece[None], (count, *piece.shape)), axes...  9.43 us
    pallas_call x1, Pallas kernels, basis(): pl.pallas_call(functools.partial(basis_kernel, root), out_shape=jax.Shape...  7.06 us
  transfers between devices with their start and end apart: 3, of which 3 were waited for; matrix products, arithmetic and copies ran while one was open for 1% of the time, Pallas kernels for 0%

profile of v4, /device:TPU:1, one launch (start us, length us, event | category | flops | bytes accessed | tf_op | source)
XLA Modules:
  0.0 133.4 jit_solution(1219972955672323121)
XLA Ops:
  0.6 2.4 %forward_tiles.1 = f32[32,8,128]{2,1,0:T(8,128)} custom-call(bf16[128,1024]{1,0:T(8,128)(2,1)} %far_jacobian.1, bf16[2,1024,128]{2,1,0:T(8,128)(2,1)} %far_probes.1, f32[8,128]{1,0:T(8,128)} %bitcast.14, f32[1,128]{1,0:T(1,128)} %bitcast.15), custom_call_target="tpu_custom_call" | custom-call | tf_op jit(solution)/shard_map/forward_tiles/pallas_call | solution.py:152
  3.0 0.0 copy-start.1
  3.0 16.1 %all-to-all-start = ((f32[32,8,128]{2,1,0:T(8,128)}), f32[32,8,128]{2,1,0:T(8,128)S(1)}, u32[]{:S(2)}, u32[]{:S(2)}) async-start(f32[32,8,128]{2,1,0:T(8,128)} %forward_tiles.1), calls=%async_computation | async-start | bytes 262144 | tf_op jit(solution)/shard_map/all_to_all | solution.py:202
  19.1 0.8 dynamic_slice.15
  19.9 0.0 copy-done.1
  19.9 11.3 %all-to-all-done = f32[32,8,128]{2,1,0:T(8,128)S(1)} async-done(((f32[32,8,128]{2,1,0:T(8,128)}), f32[32,8,128]{2,1,0:T(8,128)S(1)}, u32[]{:S(2)}, u32[]{:S(2)}) %all-to-all-start) | async-done | bytes 131104 | tf_op jit(solution)/shard_map/all_to_all | solution.py:202
  31.2 0.7 broadcast_in_dim.6
  31.9 9.4 %all-to-all-start.1 = ((bf16[64,8,128]{2,1,0:T(8,128)(2,1)}), bf16[64,8,128]{2,1,0:T(8,128)(2,1)S(1)}, u32[]{:S(2)}, u32[]{:S(2)}) async-start(bf16[64,8,128]{2,1,0:T(8,128)(2,1)} %broadcast_in_dim.6), calls=%async_computation.1 | async-start | bytes 262144 | tf_op jit(solution)/shard_map/all_to_all | solution.py:176
  41.3 11.7 %collective-permute-start = (bf16[128,512]{1,0:T(8,128)(2,1)S(1)}, bf16[128,512]{1,0:T(8,128)(2,1)S(1)}, u32[]{:S(2)}, u32[]{:S(2)}) collective-permute-start(bf16[128,512]{1,0:T(8,128)(2,1)S(1)} %get-tuple-element.13), channel_id=1, source_target_pairs={{0,256},{256,0},{1,257},{257,1},{2,258},{258,2},{3,259},{259,3},{4... | collective-permute-start | bytes 393224 | tf_op jit(solution)/shard_map/ppermute | solution.py:200
  53.1 3.3 %all-to-all-done.1 = bf16[64,8,128]{2,1,0:T(8,128)(2,1)S(1)} async-done(((bf16[64,8,128]{2,1,0:T(8,128)(2,1)}), bf16[64,8,128]{2,1,0:T(8,128)(2,1)S(1)}, u32[]{:S(2)}, u32[]{:S(2)}) %all-to-all-start.1) | async-done | bytes 131104 | tf_op jit(solution)/shard_map/all_to_all | solution.py:176
  56.4 10.4 %collective-permute-done = bf16[128,512]{1,0:T(8,128)(2,1)S(1)} collective-permute-done((bf16[128,512]{1,0:T(8,128)(2,1)S(1)}, bf16[128,512]{1,0:T(8,128)(2,1)S(1)}, u32[]{:S(2)}, u32[]{:S(2)}) %collective-permute-start) | collective-permute-done | bytes 131104 | tf_op jit(solution)/shard_map/ppermute | solution.py:200
  66.7 0.3 convolution_convert_fusion
  67.0 12.6 %all_to_all.30 = bf16[8,64,256]{2,1,0:T(8,128)(2,1)S(1)} all-to-all(bf16[8,64,256]{2,1,0:T(8,128)(2,1)S(1)} %bitcast.12), channel_id=1, replica_groups=mesh['zh'=2,'y'=4,'c'=2,'zl'=8,'x'=4] {'y','c'}, dimensions={0} | all-to-all | bytes 524288 | tf_op jit(solution)/shard_map/all_to_all | solution.py:170
  79.6 0.1 broadcast_multiply_fusion.sketch
  79.7 0.0 copy-start
  79.7 0.3 convolution_convert_fusion.1
  80.2 13.0 %all_to_all.31 = bf16[32,4,384]{2,1,0:T(4,128)(2,1)S(1)} all-to-all(bf16[32,4,384]{2,1,0:T(4,128)(2,1)S(1)} %pad_maximum_fusion), channel_id=1, replica_groups=mesh['zh'=2,'y'=4,'c'=2,'zl'=8,'x'=4] {'y','c','x'}, dimensions={0} | all-to-all | bytes 196608 | tf_op jit(solution)/shard_map/all_to_all | solution.py:170
  93.1 0.1 convert_reduce_fusion.1
  93.2 19.6 %all_to_all.32 = bf16[16,4,384]{2,1,0:T(4,128)(2,1)S(1)} all-to-all(bf16[16,4,384]{2,1,0:T(4,128)(2,1)S(1)} %broadcast_in_dim.7), channel_id=1, replica_groups=mesh['zh'=2,'y'=4,'c'=2,'zl'=8,'x'=4] {'zh','zl'}, dimensions={0} | all-to-all | bytes 98304 | tf_op jit(solution)/shard_map/all_to_all | solution.py:176
  112.9 13.4 %all_to_all.33.packed = f32[32,4,384]{2,1,0:T(4,128)S(1)} all-to-all(f32[32,4,384]{2,1,0:T(4,128)S(1)} %broadcast_in_dim.8), channel_id=1, replica_groups=mesh['zh'=2,'y'=4,'c'=2,'zl'=8,'x'=4] {'y','c','x'}, dimensions={0} | all-to-all | bytes 393216 | tf_op jit(solution)/shard_map/all_to_all | solution.py:176
  126.4 0.0 copy-done
  126.4 7.1 %cholesky_basis.1 = f32[64,256]{1,0:T(8,128)} custom-call(f32[32,4,384]{2,1,0:T(4,128)S(1)} %all_to_all.33.packed, f32[64,256]{1,0:T(8,128)S(1)} %broadcast_multiply_fusion.sketch), custom_call_target="tpu_custom_call" | custom-call | tf_op jit(solution)/shard_map/cholesky_basis/pallas_call | solution.py:106
  (11 shorter events, 0.3 us)
Async XLA Ops:
  3.0 16.9 %copy-start.1 = (bf16[128,1024]{1,0:T(8,128)(2,1)S(1)}, bf16[128,1024]{1,0:T(8,128)(2,1)}, u32[]{:S(2)}) copy-start(bf16[128,1024]{1,0:T(8,128)(2,1)} %far_jacobian.1) | copy-start | bytes 786436
  3.0 28.2 %all-to-all-start = ((f32[32,8,128]{2,1,0:T(8,128)}), f32[32,8,128]{2,1,0:T(8,128)S(1)}, u32[]{:S(2)}, u32[]{:S(2)}) async-start(f32[32,8,128]{2,1,0:T(8,128)} %forward_tiles.1), calls=%async_computation | async-start | bytes 262144 | tf_op jit(solution)/shard_map/all_to_all | solution.py:202
  31.9 24.4 %all-to-all-start.1 = ((bf16[64,8,128]{2,1,0:T(8,128)(2,1)}), bf16[64,8,128]{2,1,0:T(8,128)(2,1)S(1)}, u32[]{:S(2)}, u32[]{:S(2)}) async-start(bf16[64,8,128]{2,1,0:T(8,128)(2,1)} %broadcast_in_dim.6), calls=%async_computation.1 | async-start | bytes 262144 | tf_op jit(solution)/shard_map/all_to_all | solution.py:176
  41.3 25.4 %collective-permute-start = (bf16[128,512]{1,0:T(8,128)(2,1)S(1)}, bf16[128,512]{1,0:T(8,128)(2,1)S(1)}, u32[]{:S(2)}, u32[]{:S(2)}) collective-permute-start(bf16[128,512]{1,0:T(8,128)(2,1)S(1)} %get-tuple-element.13), channel_id=1, source_target_pairs={{0,256},{256,0},{1,257},{257,1},{2,258},{258,2},{3,259},{259,3},{4... | collective-permute-start | bytes 393224 | tf_op jit(solution)/shard_map/ppermute | solution.py:200
  79.7 46.6 %copy-start = (f32[64,256]{1,0:T(8,128)}, f32[64,256]{1,0:T(8,128)S(1)}, u32[]{:S(2)}) copy-start(f32[64,256]{1,0:T(8,128)S(1)} %broadcast_multiply_fusion.sketch) | copy-start | bytes 196612
